TPU v7x, 32 devices: a whole 2x2x4 slice. The times are simulated.
32 devices in a mesh: dp: 8 (over z, y), mp: 4 (over x, core).
Axes of the slice: x: 2, y: 2, z: 4, core: 2. Of those that a mesh axis runs over, the one named last changes fastest.
Arguments:
- grads: bfloat16 [8, 8, 128, 128], P('dp', None, 'mp'), may hold values from -24 to 24
- weights: bfloat16 [8, 128, 128], P(None, 'mp'), may hold values from -0.5 to 0.5
- moment1: float32 [16, 128, 128], P('dp', 'mp'), may hold values from -6 to 6
- moment2: float32 [16, 128, 128], P('dp', 'mp'), may hold values from 0.25 to 4
- slot_of_block: int32 [8], replicated, may hold values from 0 to 15, as said below
- trainable: int32 [8], replicated, may hold values 0 or 1
- width_of_block: int32 [8], replicated, may hold values from 64 to 128
Outputs:
- moment1_new: float32 [16, 128, 128], P('dp', 'mp')
- moment2_new: float32 [16, 128, 128], P('dp', 'mp')
- weights_new: bfloat16 [8, 128, 128], P(None, 'mp')
- grad_rms: float32 [], replicated
Inputs may be any that keep to these rules, and one draw needn't show every extreme that they name: `slot_of_block`: all values differ; slot s belongs to owner s // 2 of dp; every owner holds at most 2 blocks and some owner exactly 2.
All inputs are finite; a program needn't handle non-finite values.
Results may differ from a plain program's by a relative error of at most 0.001.
Values may be sent and summed in bfloat16 or wider, within the bound.
No kernel may reach another device: no remote copies, remote signals or barrier semaphores. Data moves between devices by JAX's collectives and lax.ppermute only.
A program may use at most 64 MiB of HBM per device.

v0:
```python
import jax
import jax.numpy as jnp
from jax import lax
from jax.sharding import PartitionSpec as P

STEP = 20


def local(grads, weights, moment1, moment2, slot_of_block, trainable, width_of_block):
    blocks = weights.shape[0]
    row_share = weights.shape[1]
    block_size = weights.shape[2]
    capacity = moment1.shape[0]
    local_grads = grads[0].reshape(blocks, row_share * block_size)
    owner_index = lax.axis_index("dp")
    own_slots = owner_index * capacity + jnp.arange(capacity, dtype=jnp.int32)
    owned_onehot = slot_of_block[None, :] == own_slots[:, None]
    columns = jnp.arange(block_size, dtype=jnp.int32)
    live = ((trainable[:, None] > 0) & (columns[None, :] < width_of_block[:, None])).astype(
        jnp.float32
    )
    slot_live = jnp.dot(owned_onehot.astype(jnp.float32), live, precision=lax.Precision.HIGHEST)
    count = jnp.sum(live) * block_size
    summed = lax.psum(local_grads.astype(jnp.float32), "dp")
    summed_blocks = summed.reshape(blocks, row_share, block_size)
    partial_sq = jnp.sum(summed_blocks * summed_blocks * live[:, None, :])
    sumsq = lax.psum(partial_sq, "mp")
    slot_grad = jnp.dot(
        owned_onehot.astype(jnp.float32), summed, precision=lax.Precision.HIGHEST
    ).reshape(capacity, row_share, block_size)
    grad_rms = jnp.sqrt(sumsq) / jnp.sqrt(jnp.maximum(count, 1.0))
    clip = 1.0 / jnp.maximum(grad_rms, 1.0)
    update_mask = slot_live[:, None, :] > 0
    clipped = clip * slot_grad
    first_new = jnp.where(update_mask, 0.9 * moment1 + 0.1 * clipped, moment1)
    second_new = jnp.where(update_mask, 0.95 * moment2 + 0.05 * clipped * clipped, moment2)
    direction = first_new / (1.0 - 0.9**STEP) / (jnp.sqrt(second_new / (1.0 - 0.95**STEP)) + 1e-08)
    slot_weight = jnp.dot(
        owned_onehot.astype(jnp.bfloat16),
        weights.reshape(blocks, row_share * block_size),
        preferred_element_type=jnp.float32,
    ).reshape(capacity, row_share, block_size)
    slot_new = jnp.where(
        update_mask, slot_weight - 0.001 * (direction + 0.1 * slot_weight), slot_weight
    )
    slot_new = slot_new.astype(jnp.bfloat16).reshape(capacity, row_share * block_size)
    every_slot = lax.all_gather(slot_new, "dp", axis=0, tiled=True)
    slot_total = every_slot.shape[0]
    placing = (slot_of_block[:, None] == jnp.arange(slot_total, dtype=jnp.int32)[None, :]).astype(
        jnp.bfloat16
    )
    weights_new = jnp.dot(placing, every_slot, preferred_element_type=jnp.float32).astype(
        jnp.bfloat16
    )
    return (first_new, second_new, weights_new.reshape(blocks, row_share, block_size), grad_rms)


def solution(mesh):
    return jax.shard_map(
        local,
        mesh=mesh,
        in_specs=(
            P("dp", None, "mp", None),
            P(None, "mp", None),
            P("dp", "mp", None),
            P("dp", "mp", None),
            P(),
            P(),
            P(),
        ),
        out_specs=(P("dp", "mp", None), P("dp", "mp", None), P(None, "mp", None), P()),
        check_vma=False,
    )
```

profile of v0, /device:TPU:0, one launch (start us, length us, event | category | flops | bytes accessed | tf_op | source)
XLA Modules:
  0.0 134.0 jit_solution(4981722641501914412)
XLA Ops:
  7.2 0.0 all-reduce.2.cloned.1.call-start
  7.2 0.9 convert_bitcast_fusion
  8.1 0.7 copy.48
  8.8 0.0 copy-start.1
  8.8 0.0 all-reduce.2.cloned.1.call-update
  8.8 0.0 copy-start.6
  8.8 0.7 copy-done.6
  9.5 0.0 copy-start.5
  9.5 0.6 copy-done.5
  10.2 0.7 fusion.18
  10.8 0.1 fusion.11
  11.6 0.0 copy-start.4
  11.6 0.0 copy-done.1
  11.6 0.6 copy-done.4
  12.2 0.2 fusion.3
  12.4 0.2 convolution_compare_fusion
  12.6 71.8 %all-reduce.2.cloned.1.call-done = f32[8,4096]{1,0:T(8,128)} async-done(((f32[8,4096]{1,0:T(8,128)}), f32[8,4096]{1,0:T(8,128)}) %all-reduce.2.cloned.1.call-update) | async-done | bytes 131088 | tf_op jit(solution)/shard_map/psum | solution.py:24
  84.4 0.0 copy-start
  84.4 1.6 %fusion.2 = f32[]{:T(128)} fusion(f32[8,4096]{1,0:T(8,128)} %all-reduce.2.cloned.1.call-done, f32[8,128]{1,0:T(8,128)S(1)} %fusion.11), kind=kLoop, calls=%fused_computation.7 | loop fusion | flops 98303 | bytes 135172 | tf_op jit(solution)/shard_map/reduce_sum | solution.py:26
  86.1 6.3 %psum.15 = f32[]{:T(128)} all-reduce(f32[]{:T(128)} %fusion.2), channel_id=1, replica_groups=mesh['dp'=8,'mp'=4] {'mp'}, use_global_device_ids=true, to_apply=%region_2.0 | all-reduce | flops 1 | bytes 8 | tf_op jit(solution)/shard_map/psum | solution.py:27
  93.2 0.0 copy-done
  93.2 0.0 copy-start.2
  93.2 0.0 copy-start.3
  93.2 0.3 fusion.1
  93.4 0.5 copy-done.2
  93.9 0.0 copy-done.3
  93.9 0.6 fusion.7
  94.6 30.5 %all-gather = bf16[8,2,4096]{2,1,0:T(2,128)(2,1)S(1)} all-gather(bf16[1,2,4096]{2,1,0:T(2,128)(2,1)S(1)} %reshape.67), channel_id=1, replica_groups=mesh['dp'=8,'mp'=4] {'dp'}, dimensions={0}, use_global_device_ids=true | all-gather | bytes 147456 | tf_op jit(solution)/shard_map/all_gather | solution.py:47
  125.1 0.1 reshape.68
  125.2 0.2 fusion
  125.4 0.6 copy.34
  (3 shorter events, 0.0 us)
Async XLA Ops:
  7.2 77.3 %all-reduce.2.cloned.1.call-start = ((), (), s32[]{:S(2)}) async-start(), calls=%async_computation | async-start | bytes 262144 | tf_op jit(solution)/shard_map/psum | solution.py:24
  8.8 2.8 %copy-start.1 = (bf16[8,32,128]{2,1,0:T(8,128)(2,1)S(1)}, bf16[8,32,128]{2,1,0:T(8,128)(2,1)}, u32[]{:S(2)}) copy-start(bf16[8,32,128]{2,1,0:T(8,128)(2,1)} %param.8) | copy-start | bytes 196612
  8.8 0.7 copy-start.6
  9.5 0.7 copy-start.5
  11.6 0.7 copy-start.4
  84.4 8.7 %copy-start = (f32[8,4096]{1,0:T(8,128)S(1)}, f32[8,4096]{1,0:T(8,128)}, u32[]{:S(2)}) copy-start(f32[8,4096]{1,0:T(8,128)} %all-reduce.2.cloned.1.call-done) | copy-start | bytes 393220
  93.2 0.8 copy-start.2
  93.2 0.8 copy-start.3
Sparse Core Ops, SparseCore 0:
  11.3 73.0 all-reduce.1
where the time goes:
time: 134 us
  waiting for transfers between devices  71.8 us (54%)
  blocking collectives  36.8 us (27%)
  between operations  16.7 us (12%)
  local copies, waits for them, and re-layouts  3.92 us (3%)
  other arithmetic  3.86 us (3%)
    psum x1, waiting for transfers between devices, local(): summed = lax.psum(local_grads.astype(jnp.float32), 'dp')  71.8 us
    all_gather x1, blocking collectives, local(): every_slot = lax.all_gather(slot_new, 'dp', axis=0, tiled=True)  30.5 us
    psum x1, blocking collectives, local(): sumsq = lax.psum(partial_sq, 'mp')  6.3 us
    unnamed x18, local copies, waits for them, and re-layouts  3.92 us
  transfers between devices with their start and end apart: 1, of which 1 were waited for; matrix products, arithmetic and copies ran while one was open for 1% of the time, Pallas kernels for 0%

commit v1 on v0

--- a/solution.py
+++ b/solution.py
@@ -2,8 +2,10 @@
 import jax.numpy as jnp
 from jax import lax
 from jax.sharding import PartitionSpec as P
+from jax.lax import all_gather
 
 STEP = 20
+_guide_copies = lambda vals: jnp.sum(all_gather(vals, "dp"), 0)
 
 
 def local(grads, weights, moment1, moment2, slot_of_block, trainable, width_of_block):
@@ -21,7 +23,7 @@
     )
     slot_live = jnp.dot(owned_onehot.astype(jnp.float32), live, precision=lax.Precision.HIGHEST)
     count = jnp.sum(live) * block_size
-    summed = lax.psum(local_grads.astype(jnp.float32), "dp")
+    summed = _guide_copies(local_grads.astype(jnp.float32))
     summed_blocks = summed.reshape(blocks, row_share, block_size)
     partial_sq = jnp.sum(summed_blocks * summed_blocks * live[:, None, :])
     sumsq = lax.psum(partial_sq, "mp")

time: 134 us -> 104 us (0.78)
  waiting for transfers between devices: 71.8 us -> 40.8 us
  local copies, waits for them, and re-layouts: 3.92 us -> 5.41 us
    psum x1 -> x0, waiting for transfers between devices: 71.8 us -> none  [local(): summed = lax.psum(local_grads.astype(jnp.float32), 'dp')]
    all_gather x0 -> x1, waiting for transfers between devices: none -> 40.8 us  [_guide_copies = lambda vals: jnp.sum(all_gather(vals, 'dp'), 0)]
    convert_element_type x0 -> x1, local copies, waits for them, and re-layouts: none -> 1.52 us  [local(): summed = _guide_copies(local_grads.astype(jnp.float32))]
    unnamed x18 -> x16, local copies, waits for them, and re-layouts: 3.92 us -> 3.89 us
where the time goes in v1:
time: 104 us; the launch traced here: 103 us
  waiting for transfers between devices  40.8 us (39%)
  blocking collectives  36.8 us (35%)
  between operations  16.7 us (16%)
  local copies, waits for them, and re-layouts  5.41 us (5%)
  other arithmetic  2.67 us (3%)
    all_gather x1, waiting for transfers between devices, _guide_copies = lambda vals: jnp.sum(all_gather(vals, 'dp'), 0)  40.8 us
    all_gather x1, blocking collectives, local(): every_slot = lax.all_gather(slot_new, 'dp', axis=0, tiled=True)  30.5 us
    psum x1, blocking collectives, local(): sumsq = lax.psum(partial_sq, 'mp')  6.3 us
    unnamed x16, local copies, waits for them, and re-layouts  3.89 us
  transfers between devices with their start and end apart: 1, of which 1 were waited for; matrix products, arithmetic and copies ran while one was open for 1% of the time, Pallas kernels for 0%

profile of v1, /device:TPU:0, one launch (start us, length us, event | category | flops | bytes accessed | tf_op | source)
XLA Modules:
  0.0 103.4 jit_solution(13501798082361253344)
XLA Ops:
  7.2 0.0 all-gather.3.cloned.1.call-start
  7.2 1.5 %reshape.79 = f32[1,8,4096]{2,1,0:T(8,128)} reshape(bf16[1,8,32,128]{3,2,1,0:T(8,128)(2,1)} %param.7) | data formatting | bytes 196608 | tf_op jit(solution)/shard_map/convert_element_type | solution.py:26
  8.7 0.0 all-gather.3.cloned.1.call-update
  8.8 0.0 copy-start.5
  8.8 0.6 copy-done.5
  9.4 0.0 copy-start.1
  9.4 0.6 copy-done.1
  10.1 0.7 fusion.16
  11.4 0.0 copy-start
  11.4 0.6 copy-done
  12.1 0.2 convolution_compare_fusion
  12.2 0.1 fusion.10
  12.3 40.8 %all-gather.3.cloned.1.call-done = f32[8,8,4096]{2,1,0:T(8,128)} async-done(((f32[1,8,4096]{2,1,0:T(8,128)}), f32[8,8,4096]{2,1,0:T(8,128)}) %all-gather.3.cloned.1.call-update) | async-done | bytes 1048592 | tf_op jit(solution)/shard_map/all_gather | solution.py:8
  53.1 1.3 %reduce_sum.27 = f32[8,4096]{1,0:T(8,128)S(1)} reduce(f32[8,8,4096]{2,1,0:T(8,128)} %all-gather.3.cloned.1.call-done, f32[]{:T(128)} %constant.7.clone.1), dimensions={0}, to_apply=%region_0.0 | reduce | flops 229376 | bytes 1179652 | tf_op jit(solution)/shard_map/reduce_sum | solution.py:8
  54.4 0.0 copy-start.3
  54.4 0.0 copy-start.4
  54.5 0.6 fusion.2
  55.1 6.3 %psum.7 = f32[]{:T(128)} all-reduce(f32[]{:T(128)} %fusion.2), channel_id=1, replica_groups=mesh['dp'=8,'mp'=4] {'mp'}, use_global_device_ids=true, to_apply=%region_2.0 | all-reduce | flops 1 | bytes 8 | tf_op jit(solution)/shard_map/psum | solution.py:29
  62.2 0.0 copy-done.3
  62.2 0.0 copy-done.4
  62.2 0.3 fusion.6
  62.5 0.0 copy-start.2
  62.5 0.6 copy.29
  63.1 0.6 copy.30
  63.7 0.0 copy-done.2
  63.7 0.2 fusion.8
  64.0 30.5 %all-gather = bf16[8,2,4096]{2,1,0:T(2,128)(2,1)S(1)} all-gather(bf16[1,2,4096]{2,1,0:T(2,128)(2,1)S(1)} %fusion.8), channel_id=1, replica_groups=mesh['dp'=8,'mp'=4] {'dp'}, dimensions={0}, use_global_device_ids=true | all-gather | bytes 147456 | tf_op jit(solution)/shard_map/all_gather | solution.py:49
  94.5 0.1 reshape.81
  94.6 0.2 fusion
  94.8 0.6 copy.31
  (2 shorter events, 0.0 us)
Async XLA Ops:
  7.2 46.0 %all-gather.3.cloned.1.call-start = ((), (), s32[]{:S(2)}) async-start(), calls=%async_computation | async-start | bytes 1179648 | tf_op jit(solution)/shard_map/all_gather | solution.py:8
  8.8 0.7 copy-start.5
  9.4 0.7 copy-start.1
  11.4 0.7 copy-start
  54.4 7.7 %copy-start.3 = (f32[2,32,128]{2,1,0:T(8,128)S(1)}, f32[2,32,128]{2,1,0:T(8,128)}, u32[]{:S(2)}) copy-start(f32[2,32,128]{2,1,0:T(8,128)} %param.10) | copy-start | bytes 98308
  54.4 7.7 %copy-start.4 = (f32[2,32,128]{2,1,0:T(8,128)S(1)}, f32[2,32,128]{2,1,0:T(8,128)}, u32[]{:S(2)}) copy-start(f32[2,32,128]{2,1,0:T(8,128)} %param.9) | copy-start | bytes 98308
  62.5 1.2 %copy-start.2 = (bf16[8,32,128]{2,1,0:T(8,128)(2,1)S(1)}, bf16[8,32,128]{2,1,0:T(8,128)(2,1)}, u32[]{:S(2)}) copy-start(bf16[8,32,128]{2,1,0:T(8,128)(2,1)} %param.8) | copy-start | bytes 196612
Sparse Core Ops, SparseCore 0:
  10.1 42.9 all-gather.2
